TPU v7x, 32 devices: a whole 2x2x4 slice. The times are simulated.
32 devices in a mesh: grp: 4 (over z), fsdp: 4 (over y, x), tp: 2 (over core).
Axes of the slice: x: 2, y: 2, z: 4, core: 2. Of those that a mesh axis runs over, the one named last changes fastest.
Arguments:
- frames: bfloat16 [768, 5120], P('fsdp', 'grp'), may hold values from -6 to 6
- projector: bfloat16 [5120, 8192], P('grp', 'tp'), may hold values from -0.078125 to 0.078125
- text_token_embedding: bfloat16 [4096, 8192], P(('grp', 'fsdp'), 'tp'), may hold values from -6 to 6
- norm_gain_vector: float32 [8192], replicated, may hold values from 0.1 to 1.9
- frozen: bfloat16 [8192, 1024], P('fsdp', 'tp'), may hold values from -0.0625 to 0.0625
- adapter_down_map: bfloat16 [8192, 64], P('fsdp'), may hold values from -0.0625 to 0.0625
- adapter_up_map: bfloat16 [64, 1024], P(None, 'tp'), may hold values from -0.75 to 0.75
- clip_frame_length: int32 [4, 4, 4], P('fsdp'), may hold values from 1 to 24, as said below
- audio_first_token: int32 [4, 4, 4], P('fsdp'), may hold values from 0 to 255, as said below
- segment_document_index: int32 [4096], P(('grp', 'fsdp')), may hold values from 0 to 63, never falling along the last dimension, each value on 1 to 256 neighbouring positions
- keep_document_flags: int32 [64], replicated, may hold values 0 or 1
- cotangent: bfloat16 [4096, 1024], P(('grp', 'fsdp'), 'tp'), may hold values from -0.09375 to 0.09375
Outputs:
- value_output: bfloat16 [4096, 1024], P(('grp', 'fsdp'), 'tp')
- projector_grad: float32 [5120, 8192], P('grp', 'tp')
- down_map_gradient: float32 [8192, 64], P('tp')
- up_map_gradient: float32 [64, 1024], P(None, 'tp')
Inputs may be any that keep to these rules, and one draw needn't show every extreme that they name: `clip_frame_length`: entry [f, g, k] is the length of clip k of frame block f * 4 + g; the 4 clips of a block sum to 48, and one of them has exactly 24 frames. `audio_first_token`: entry [f, g, k] is the first token, among the 256 tokens of block k * 4 + f, of the audio slots of clip k of frame block f * 4 + g; the 4 clips that one token block takes lie in distinct aligned windows of 64 tokens.
All inputs are finite; a program needn't handle non-finite values.
Results may differ from a plain program's by a relative error of at most 0.018.
Values may be sent and summed in bfloat16 or wider, within the bound.
A program may use at most 128 MiB of HBM per device.

v0:
```python
import jax
import jax.numpy as jnp
from jax import lax
from jax.sharding import PartitionSpec as P

adapter_scale = 2.0
norm_eps = 1e-05
plane = ("fsdp", "tp")


def contract_leading(left_side, right_side):
    return lax.dot_general(
        left_side, right_side, (((0,), (0,)), ((), ())), preferred_element_type=jnp.float32
    )


def contract_trailing(left_side, right_side):
    return lax.dot_general(
        left_side, right_side, (((1,), (1,)), ((), ())), preferred_element_type=jnp.float32
    )


def block_perm(f_size, t_size, shift):
    pairs = []
    for f_src in range(f_size):
        for t_src in range(t_size):
            b = f_src * t_size + (t_src + shift) % t_size
            pairs.append((f_src * t_size + t_src, b % f_size * t_size + b // f_size))
    return pairs


def shards(
    frames,
    projector,
    text_token_embedding,
    norm_gain_vector,
    frozen,
    adapter_down_map,
    adapter_up_map,
    clip_frame_length,
    audio_first_token,
    segment_document_index,
    keep_document_flags,
    cotangent,
):
    g_idx, f_idx, t_idx = (lax.axis_index("grp"), lax.axis_index("fsdp"), lax.axis_index("tp"))
    f_size, t_size = (lax.axis_size("fsdp"), lax.axis_size("tp"))
    tok, width = text_token_embedding.shape
    groups = clip_frame_length.shape[1]
    block_frames = frames.shape[0]
    per_group = block_frames // groups
    cols = width // f_size
    full_width = width * t_size
    v_shard = frozen.shape[1]
    v_full = v_shard * t_size
    rank = adapter_down_map.shape[1]
    frames_all = lax.all_gather(frames, "fsdp", axis=0, tiled=True)
    clips = lax.all_gather(jnp.stack([clip_frame_length[0], audio_first_token[0]]), "fsdp", axis=0)
    text = lax.all_to_all(
        text_token_embedding.reshape(tok, f_size, cols).transpose(1, 0, 2),
        "fsdp",
        split_axis=0,
        concat_axis=0,
        tiled=True,
    )
    own_block = t_idx * f_size + f_idx
    own_j = lax.rem(own_block, t_size)
    frozen_own = jnp.zeros((cols, v_full), jnp.bfloat16)
    for shift in range(t_size):
        j = lax.rem(t_idx + shift, t_size)
        piece = lax.ppermute(
            lax.dynamic_slice_in_dim(frozen, j * cols, cols, 0),
            plane,
            block_perm(f_size, t_size, shift),
        )
        t_src = lax.rem(own_j - shift + t_size, t_size)
        frozen_own = lax.dynamic_update_slice_in_dim(frozen_own, piece, t_src * v_shard, 1)
    down_own = lax.ppermute(
        lax.dynamic_slice_in_dim(adapter_down_map, t_idx * cols, cols, 0),
        plane,
        block_perm(f_size, t_size, 0),
    )
    gain_own = lax.dynamic_slice_in_dim(norm_gain_vector, t_idx * width + f_idx * cols, cols, 0)
    sizes, firsts = (clips[:, 0], clips[:, 1])
    ends = jnp.cumsum(sizes, axis=2)
    pick = lax.broadcasted_iota(jnp.int32, sizes.shape, 2) == g_idx
    size_in = jnp.sum(jnp.where(pick, sizes, 0), axis=2)
    start_in = jnp.sum(jnp.where(pick, ends - sizes, 0), axis=2)
    first_in = jnp.sum(jnp.where(pick, firsts, 0), axis=2)
    base_row = lax.broadcasted_iota(jnp.int32, size_in.shape, 1) * per_group + start_in
    token_iota = lax.broadcasted_iota(jnp.int32, (f_size, tok, groups), 1)
    offset = token_iota - first_in[:, None, :]
    live = (offset >= 0) & (offset < size_in[:, None, :])
    is_audio = jnp.any(live, axis=2)
    row = jnp.sum(jnp.where(live, base_row[:, None, :] + offset, 0), axis=2)
    row = jnp.where(is_audio, row, -1)
    frame_iota = lax.broadcasted_iota(jnp.int32, (f_size, tok, block_frames), 2)
    take = (row[:, :, None] == frame_iota).astype(jnp.bfloat16)
    take_own = lax.dynamic_index_in_dim(take, f_idx, 0, keepdims=False)
    doc_iota = lax.broadcasted_iota(jnp.int32, (tok, keep_document_flags.shape[0]), 1)
    weight_tok = jnp.sum(
        jnp.where(segment_document_index[:, None] == doc_iota, keep_document_flags[None, :], 0),
        axis=1,
    )
    grad_out = cotangent * weight_tok.astype(jnp.bfloat16)[:, None]
    both = lax.all_gather(
        jnp.concatenate([grad_out, adapter_up_map], axis=0), "tp", axis=1, tiled=True
    )
    grad_full, up_full = (both[:tok], both[tok:])
    lora_tok = (adapter_scale * contract_trailing(grad_full, up_full)).astype(jnp.bfloat16)
    lora_plane = lax.all_gather(lora_tok, "fsdp", axis=0, tiled=True)
    grad_rows = lax.psum(contract_leading(take_own, grad_full).astype(jnp.bfloat16), "grp")
    grad_rows = lax.all_gather(grad_rows, "fsdp", axis=0, tiled=True)
    lora_rows = (adapter_scale * contract_trailing(grad_rows, up_full)).astype(jnp.bfloat16)
    grad_norm = contract_trailing(grad_rows, frozen_own) + contract_trailing(lora_rows, down_own)
    projector_own = lax.dynamic_slice_in_dim(projector, f_idx * cols, cols, 1)
    embedded = lax.psum(
        jnp.dot(frames_all, projector_own, preferred_element_type=jnp.float32).astype(jnp.bfloat16),
        "grp",
    )
    audio = lax.dot_general(
        take,
        embedded.reshape(f_size, block_frames, cols),
        (((2,), (1,)), ((0,), (0,))),
        preferred_element_type=jnp.float32,
    ).astype(jnp.bfloat16)
    x = jnp.where(is_audio[:, :, None], audio, text).reshape(f_size * tok, cols)
    x32 = x.astype(jnp.float32)
    e32 = embedded.astype(jnp.float32)
    stats = lax.psum(
        jnp.concatenate(
            [
                jnp.sum(x32 * x32, axis=1),
                jnp.sum(e32 * e32, axis=1),
                jnp.sum(e32 * gain_own[None, :] * grad_norm, axis=1),
            ]
        ),
        plane,
    )
    n_tok, n_frames = (f_size * tok, f_size * block_frames)
    inv_tok = lax.rsqrt(stats[:n_tok] / full_width + norm_eps)
    inv_frame = lax.rsqrt(stats[n_tok : n_tok + n_frames] / full_width + norm_eps)
    dots = inv_frame * stats[n_tok + n_frames :]
    frame_grad = (
        inv_frame[:, None] * gain_own[None, :] * grad_norm
        - e32 * (inv_frame * inv_frame * dots / full_width)[:, None]
    ).astype(jnp.bfloat16)
    frame_grad = lax.all_gather(frame_grad, "fsdp", axis=1, tiled=True)
    projector_grad = contract_leading(frames_all, frame_grad)
    normed = (x32 * inv_tok[:, None] * gain_own[None, :]).astype(jnp.bfloat16)
    low_part = jnp.dot(normed, down_own, preferred_element_type=jnp.float32)
    value_part = jnp.dot(normed, frozen_own, preferred_element_type=jnp.float32)
    value_part = value_part + adapter_scale * jnp.dot(
        low_part.astype(jnp.bfloat16), up_full, preferred_element_type=jnp.float32
    )
    value_part = value_part.astype(jnp.bfloat16).reshape(f_size, tok, t_size, v_shard)
    low_send = jnp.broadcast_to(
        low_part.astype(jnp.bfloat16).reshape(f_size, tok, 1, rank), (f_size, tok, t_size, rank)
    )
    sent = (
        jnp.concatenate([value_part, low_send], axis=3)
        .transpose(0, 2, 1, 3)
        .reshape(f_size * t_size, tok, v_shard + rank)
    )
    got = lax.all_to_all(sent, plane, split_axis=0, concat_axis=0, tiled=True)
    total = jnp.sum(got.astype(jnp.float32), axis=0)
    value_output = total[:, :v_shard].astype(jnp.bfloat16)
    low_half = total[:, v_shard:].astype(jnp.bfloat16)
    up_part = adapter_scale * contract_leading(low_half, grad_out)
    down_part = contract_leading(normed, lora_plane)
    down_sum, up_sum = lax.psum((down_part, up_part), "grp")
    gathered = lax.all_gather(
        jnp.concatenate([down_sum, up_sum.reshape(-1, rank)], axis=0), "fsdp", axis=0
    )
    down_map_gradient = gathered[:, :cols].reshape(width, rank)
    up_map_gradient = jnp.sum(gathered[:, cols:], axis=0).reshape(rank, v_shard)
    return (value_output, projector_grad, down_map_gradient, up_map_gradient)


def solution(mesh):
    in_specs = (
        P("fsdp", "grp"),
        P("grp", "tp"),
        P(("grp", "fsdp"), "tp"),
        P(),
        P("fsdp", "tp"),
        P("fsdp", None),
        P(None, "tp"),
        P("fsdp", None, None),
        P("fsdp", None, None),
        P(("grp", "fsdp")),
        P(),
        P(("grp", "fsdp"), "tp"),
    )
    out_specs = (P(("grp", "fsdp"), "tp"), P("grp", "tp"), P("tp", None), P(None, "tp"))
    return jax.shard_map(shards, mesh=mesh, in_specs=in_specs, out_specs=out_specs, check_vma=False)
```

profile of v0, /device:TPU:0, one launch (start us, length us, event | category | flops | bytes accessed | tf_op | source)
XLA Modules:
  0.0 499.5 jit_solution(9193602135876863072)
XLA Ops:
  9.5 9.7 %all-gather = s32[8,4,4]{2,1,0:T(4,128)S(1)} all-gather(s32[2,4,4]{2,1,0:T(4,128)S(1)} %pad_add_fusion), channel_id=2, replica_groups=mesh['grp'=4,'fsdp'=4,'tp'=2] {'fsdp'}, dimensions={0}, use_global_device_ids=true | all-gather | bytes 640 | tf_op jit(solution)/shard_map/all_gather | solution.py:58
  25.8 20.9 %all-gather.7.cloned.1.call-done = bf16[768,1280]{1,0:T(8,128)(2,1)} async-done(((bf16[192,1280]{1,0:T(8,128)(2,1)}), bf16[768,1280]{1,0:T(8,128)(2,1)}) %all-gather.7.cloned.1.call-update) | async-done | bytes 1966096 | tf_op jit(solution)/shard_map/all_gather | solution.py:57
  46.7 5.7 %fusion.12 = bf16[768,1024]{0,1:T(8,128)(2,1)} fusion(bf16[768,1280]{1,0:T(8,128)(2,1)} %all-gather.7.cloned.1.call-done, bf16[1280,4096]{1,0:T(8,128)(2,1)} %param.13, s32[]{:T(128)S(6)} %select_n.60), kind=kOutput, calls=%fused_computation.20 | convolution fusion | flops 2014052352 | bytes 6160388 | tf_op jit(solution)/shard_map/dot_general | solution.py:118
  52.5 82.0 %all-reduce.7.cloned.1.call-done = (bf16[768,1024]{0,1:T(8,128)(2,1)}, bf16[192,1024]{1,0:T(8,128)(2,1)}) async-done(((bf16[768,1024]{0,1:T(8,128)(2,1)}, bf16[192,1024]{1,0:T(8,128)(2,1)}), (bf16[768,1024]{0,1:T(8,128)(2,1)}, bf16[192,1024]{1,0:T(8,128)(2,1)})) %all-reduce.7.cloned.1.call-update) | async-done | bytes 1966096 | tf_op jit(solution)/shard_map/psum | solution.py:117
  134.5 3.3 copy.56
  140.2 3.6 all-to-all-start
  146.8 9.4 %collective-permute-start = (bf16[1024,512]{1,0:T(8,128)(2,1)}, bf16[1024,512]{1,0:T(8,128)(2,1)}, u32[]{:S(2)}, u32[]{:S(2)}) collective-permute-start(bf16[1024,512]{1,0:T(8,128)(2,1)} %get-tuple-element.30), channel_id=1, source_target_pairs={{0,0},{1,2},{2,4},{3,6},{4,1},{5,3},{6,5},{7,7},{8,8},{9,10},{10,1... | collective-permute-start | bytes 3145736 | tf_op jit(solution)/shard_map/ppermute | solution.py:71
  161.6 40.1 %collective-permute-done.1 = bf16[1024,512]{1,0:T(8,128)(2,1)} collective-permute-done((bf16[1024,512]{1,0:T(8,128)(2,1)}, bf16[1024,512]{1,0:T(8,128)(2,1)}, u32[]{:S(2)}, u32[]{:S(2)}) %collective-permute-start.1) | collective-permute-done | bytes 1048608 | tf_op jit(solution)/shard_map/ppermute | solution.py:71
  206.6 4.5 multiply_reduce_fusion
  211.2 4.3 fusion.16
  215.5 6.7 %fusion.2 = (f32[768]{0:T(1024)S(1)}, f32[768]{0:T(1024)S(1)}, f32[768,1024]{0,1:T(8,128)}) fusion(bf16[768,1024]{0,1:T(8,128)(2,1)S(1)} %copy-done.2, f32[1024]{0:T(1024)S(1)} %dynamic_slice.20, f32[768,1024]{0,1:T(8,128)} %fusion.16, bf16[768,1024]{1,0:T(8,128)(2,1)} %all-gather.9.cloned.1.call-done, bf16[1024,1024]{1,0:T(8,128)(2,1)} %constant_dynamic-update-slice_fusion), kind=kOutput, calls=%fused_computation.9 | convolution fusion | flops 1616116224 | bytes 11544576 | tf_op jit(solution)/shard_map/dot_general | solution.py:18
  222.2 27.2 %psum.37 = f32[2560]{0:T(1024)S(1)} all-reduce(f32[2560]{0:T(1024)S(1)} %pad_maximum_fusion.3), channel_id=1, replica_groups=mesh['grp'=4,'fsdp'=4,'tp'=2] {'fsdp','tp'}, use_global_device_ids=true, to_apply=%region_12.13 | all-reduce | flops 2560 | bytes 20480 | tf_op jit(solution)/shard_map/psum | solution.py:130
  253.5 5.3 %add_convert_fusion = bf16[1024,1024]{1,0:T(8,128)(2,1)} fusion(f32[1024,1024]{1,0:T(8,128)S(1)} %fusion.23, bf16[1024,1024]{1,0:T(8,128)(2,1)S(1)} %fusion.1, bf16[1024,1024]{1,0:T(8,128)(2,1)} %constant_dynamic-update-slice_fusion), kind=kOutput, calls=%fused_computation.7 | convolution fusion | flops 2150629376 | bytes 10485760 | tf_op jit(solution)/shard_map/dot_general | solution.py:152
  258.7 4.5 reshape.66
  263.2 6.1 %copy.61 = bf16[4,256,2,512]{1,3,2,0:T(8,128)(2,1)} copy(bf16[4,256,2,512]{3,2,1,0:T(2,128)(2,1)} %reshape.66) | data formatting | bytes 4194304 | tf_op jit(solution)/shard_map/reshape | solution.py:156
  269.4 3.2 pad_maximum_fusion
  272.5 4.4 all-to-all-start.1
  277.2 32.5 %all_gather.33 = bf16[1024,64]{0,1:T(8,128)(2,1)S(1)} all-gather(bf16[256,64]{0,1:T(8,128)(2,1)S(1)} %fusion.17), channel_id=1, replica_groups=mesh['grp'=4,'fsdp'=4,'tp'=2] {'fsdp'}, dimensions={0}, use_global_device_ids=true | all-gather | bytes 163840 | tf_op jit(solution)/shard_map/all_gather | solution.py:111
  314.3 35.8 %all-reduce.5.cloned.1.call-done = (f32[512,64]{0,1:T(8,128)}, f32[1024,64]{0,1:T(8,128)}) async-done(((f32[512,64]{0,1:T(8,128)}, f32[1024,64]{0,1:T(8,128)}), (f32[512,64]{0,1:T(8,128)}, f32[1024,64]{0,1:T(8,128)})) %all-reduce.5.cloned.1.call-update) | async-done | bytes 393232 | tf_op jit(solution)/shard_map/psum | solution.py:171
  352.2 3.6 fusion.6
  356.7 26.3 %all-gather.13.cloned.1.call-done = f32[6144,64]{0,1:T(8,128)} async-done(((f32[1536,64]{0,1:T(8,128)}), f32[6144,64]{0,1:T(8,128)}) %all-gather.13.cloned.1.call-update) | async-done | bytes 1572880 | tf_op jit(solution)/shard_map/all_gather | solution.py:172
  388.3 67.0 %all-gather.11.cloned.1.call-done = bf16[768,4096]{0,1:T(8,128)(2,1)} async-done(((bf16[768,1024]{0,1:T(8,128)(2,1)}), bf16[768,4096]{0,1:T(8,128)(2,1)}) %all-gather.11.cloned.1.call-update) | async-done | bytes 6291472 | tf_op jit(solution)/shard_map/all_gather | solution.py:148
  455.3 14.9 %convolution_bitcast_fusion = f32[1280,4096]{0,1:T(8,128)} fusion(bf16[768,4096]{0,1:T(8,128)(2,1)} %all-gather.11.cloned.1.call-done, bf16[768,1280]{1,0:T(8,128)(2,1)} %all-gather.7.cloned.1.call-done), kind=kOutput, calls=%fused_computation | convolution fusion | flops 8053063680 | bytes 29229056 | tf_op jit(solution)/shard_map/dot_general | solution.py:12
  470.2 22.4 %copy.65 = f32[1280,4096]{1,0:T(8,128)} copy(f32[1280,4096]{0,1:T(8,128)} %convolution_bitcast_fusion) | data formatting | bytes 41943040
  (78 shorter events, 41.8 us)
Async XLA Ops:
  7.2 149.1 %copy-start = (bf16[2048,64]{0,1:T(8,128)(2,1)S(1)}, bf16[2048,64]{0,1:T(8,128)(2,1)}, u32[]{:S(2)}) copy-start(bf16[2048,64]{0,1:T(8,128)(2,1)} %param.17) | copy-start | bytes 786436
  7.2 39.5 %all-gather.7.cloned.1.call-start = ((), (), s32[]{:S(2)}) async-start(), calls=%async_computation.2 | async-start | bytes 2457600 | tf_op jit(solution)/shard_map/all_gather | solution.py:57
  7.9 126.6 %all-reduce.7.cloned.1.call-start = ((), (), s32[]{:S(2)}) async-start(), calls=%async_computation.7 | async-start | bytes 3932160 | tf_op jit(solution)/shard_map/psum | solution.py:117
  52.5 158.7 %all-gather.9.cloned.1.call-start = ((), (), s32[]{:S(2)}) async-start(), calls=%async_computation.3 | async-start | bytes 1966080 | tf_op jit(solution)/shard_map/all_gather | solution.py:113
  140.2 66.4 %all-to-all-start = ((bf16[4,256,1024]{2,1,0:T(8,128)(2,1)}), bf16[4,256,1024]{2,1,0:T(8,128)(2,1)S(1)}, u32[]{:S(2)}, u32[]{:S(2)}) async-start(bf16[4,256,1024]{2,1,0:T(8,128)(2,1)} %bitcast.60), calls=%async_computation | async-start | bytes 4194304 | tf_op jit(solution)/shard_map/all_to_all | solution.py:59
  146.8 10.9 %collective-permute-start = (bf16[1024,512]{1,0:T(8,128)(2,1)}, bf16[1024,512]{1,0:T(8,128)(2,1)}, u32[]{:S(2)}, u32[]{:S(2)}) collective-permute-start(bf16[1024,512]{1,0:T(8,128)(2,1)} %get-tuple-element.30), channel_id=1, source_target_pairs={{0,0},{1,2},{2,4},{3,6},{4,1},{5,3},{6,5},{7,7},{8,8},{9,10},{10,1... | collective-permute-start | bytes 3145736 | tf_op jit(solution)/shard_map/ppermute | solution.py:71
  156.3 45.4 %collective-permute-start.1 = (bf16[1024,512]{1,0:T(8,128)(2,1)}, bf16[1024,512]{1,0:T(8,128)(2,1)}, u32[]{:S(2)}, u32[]{:S(2)}) collective-permute-start(bf16[1024,512]{1,0:T(8,128)(2,1)} %get-tuple-element.29), channel_id=1, source_target_pairs={{0,2},{1,0},{2,6},{3,4},{4,3},{5,1},{6,7},{7,5},{8,10},{9,8},{10,1... | collective-permute-start | bytes 3145736 | tf_op jit(solution)/shard_map/ppermute | solution.py:71
  156.3 54.8 %collective-permute-start.2 = (bf16[1024,64]{0,1:T(8,128)(2,1)S(1)}, bf16[1024,64]{0,1:T(8,128)(2,1)S(1)}, u32[]{:S(2)}, u32[]{:S(2)}) collective-permute-start(bf16[1024,64]{0,1:T(8,128)(2,1)S(1)} %constant_dynamic-slice_fusion.2), channel_id=1, source_target_pairs={{0,0},{1,2},{2,4},{3,6},{4,1},{5,3},{6,5},{7,7},{8,8},{9,10},{10,1... | collective-permute-start | bytes 393224 | tf_op jit(solution)/shard_map/ppermute | solution.py:78
  211.1 4.3 copy-start.2
  272.5 38.4 %all-to-all-start.1 = ((bf16[8,256,576]{1,2,0:T(8,128)(2,1)}), bf16[8,256,576]{1,2,0:T(8,128)(2,1)}, u32[]{:S(2)}, u32[]{:S(2)}) async-start(bf16[8,256,576]{1,2,0:T(8,128)(2,1)} %bitcast.59), calls=%async_computation.1 | async-start | bytes 4718592 | tf_op jit(solution)/shard_map/all_to_all | solution.py:165
  276.9 73.2 %all-reduce.5.cloned.1.call-start = ((), (), s32[]{:S(2)}) async-start(), calls=%async_computation.6 | async-start | bytes 786432 | tf_op jit(solution)/shard_map/psum | solution.py:171
  310.9 41.2 %copy-start.3 = (bf16[768,1024]{0,1:T(8,128)(2,1)S(1)}, bf16[768,1024]{0,1:T(8,128)(2,1)}, u32[]{:S(2)}) copy-start(bf16[768,1024]{0,1:T(8,128)(2,1)} %get-tuple-element.27) | copy-start | bytes 4718596
  314.3 68.8 %all-gather.13.cloned.1.call-start = ((), (), s32[]{:S(2)}) async-start(), calls=%async_computation.5 | async-start | bytes 1966080 | tf_op jit(solution)/shard_map/all_gather | solution.py:172
  351.9 103.4 %all-gather.11.cloned.1.call-start = ((), (), s32[]{:S(2)}) async-start(), calls=%async_computation.4 | async-start | bytes 7864320 | tf_op jit(solution)/shard_map/all_gather | solution.py:148
  470.2 22.4 %copy-start.1 = (bf16[2048,64]{0,1:T(8,128)(2,1)S(1)}, bf16[2048,64]{0,1:T(8,128)(2,1)}, u32[]{:S(2)}) copy-start(bf16[2048,64]{0,1:T(8,128)(2,1)} %param.17) | copy-start | bytes 786436
Sparse Core Ops, SparseCore 0:
  9.8 36.8 all-gather.6
  52.6 81.8 all-reduce.6
  136.3 52.9 all-gather.8
  314.4 35.6 all-reduce.4
  352.3 30.6 all-gather.12
  385.3 70.0 all-gather.10
where the time goes:
time: 502 us; the launch traced here: 499 us
  waiting for transfers between devices  273 us (54%)
  blocking collectives  71.6 us (14%)
  local copies, waits for them, and re-layouts  58.1 us (12%)
  matrix products  45.5 us (9%)
  starting transfers between devices  18.6 us (4%)
  other arithmetic  18.5 us (4%)
  between operations  14.3 us (3%)
    psum x1, waiting for transfers between devices, shards(): lax.psum(jnp.dot(frames_all, projector_own, preferred_element_type=jnp.fl...  82 us
    all_gather x1, waiting for transfers between devices, shards(): frame_grad = lax.all_gather(frame_grad, 'fsdp', axis=1, tiled=True)  67 us
    ppermute x2, waiting for transfers between devices, shards(): lax.ppermute(lax.dynamic_slice_in_dim(frozen, j * cols, cols, 0), plane,...  40.1 us
    psum x1, waiting for transfers between devices, shards(): down_sum, up_sum = lax.psum((down_part, up_part), 'grp')  35.8 us
    all_gather x1, blocking collectives, shards(): lora_plane = lax.all_gather(lora_tok, 'fsdp', axis=0, tiled=True)  32.5 us
    unnamed x13, local copies, waits for them, and re-layouts  28.2 us
    psum x1, blocking collectives, shards(): lax.psum(jnp.concatenate([jnp.sum(x32 * x32, axis=1), jnp.sum(e32 * e32,...  27.2 us
    all_gather x1, waiting for transfers between devices, shards(): lax.all_gather(jnp.concatenate([down_sum, up_sum.reshape(-1, rank)], axis...  26.3 us
  transfers between devices with their start and end apart: 11, of which 6 were waited for; matrix products, arithmetic and copies ran while one was open for 8% of the time, Pallas kernels for 0%

commit v1 on v0

--- a/solution.py
+++ b/solution.py
@@ -1,3 +1,4 @@
+import functools
 import jax
 import jax.numpy as jnp
 from jax import lax
@@ -6,6 +7,14 @@
 adapter_scale = 2.0
 norm_eps = 1e-05
 plane = ("fsdp", "tp")
+
+
+def touch_the_racks(field, ax_name):
+    r1 = jnp.sum(jax.lax.all_gather(field, ax_name), axis=0)
+    return r1
+
+
+switch_rates_for = functools.partial(touch_the_racks, ax_name="grp")
 
 
 def contract_leading(left_side, right_side):
@@ -114,9 +123,8 @@
     lora_rows = (adapter_scale * contract_trailing(grad_rows, up_full)).astype(jnp.bfloat16)
     grad_norm = contract_trailing(grad_rows, frozen_own) + contract_trailing(lora_rows, down_own)
     projector_own = lax.dynamic_slice_in_dim(projector, f_idx * cols, cols, 1)
-    embedded = lax.psum(
-        jnp.dot(frames_all, projector_own, preferred_element_type=jnp.float32).astype(jnp.bfloat16),
-        "grp",
+    embedded = switch_rates_for(
+        jnp.dot(frames_all, projector_own, preferred_element_type=jnp.float32).astype(jnp.bfloat16)
     )
     audio = lax.dot_general(
         take,

time: 502 us -> 562 us (1.12)
  waiting for transfers between devices: 273 us -> 312 us
  other arithmetic: 18.5 us -> 28.9 us
  local copies, waits for them, and re-layouts: 58.1 us -> 67.2 us
    all_gather x0 -> x1, waiting for transfers between devices: none -> 114 us  [touch_the_racks(): r1 = jnp.sum(jax.lax.all_gather(field, ax_name), axis=0)]
    psum x1, waiting for transfers between devices: 82 us -> 36.7 us  [shards(): lax.psum(contract_leading(take_own, grad_full).astype(jnp.bfloat16), 'grp')]
    all_gather x1, waiting for transfers between devices: 20.9 us -> 0.02 us  [shards(): frames_all = lax.all_gather(frames, 'fsdp', axis=0, tiled=True)]
    all_gather x0 -> x1, local copies, waits for them, and re-layouts: none -> 12.3 us  [touch_the_racks(): r1 = jnp.sum(jax.lax.all_gather(field, ax_name), axis=0)]
    reduce_sum x0 -> x1, other arithmetic: none -> 10.4 us  [touch_the_racks(): r1 = jnp.sum(jax.lax.all_gather(field, ax_name), axis=0)]
    ppermute x2, waiting for transfers between devices: 40.1 us -> 34 us  [shards(): lax.ppermute(lax.dynamic_slice_in_dim(frozen, j * cols, cols, 0), plane,...]
    unnamed x13 -> x29, local copies, waits for them, and re-layouts: 28.2 us -> 29.2 us
  transfers between devices with their start and end apart: 11 -> 12, of which waited for: 6 -> 6; matrix products, arithmetic and copies ran while one was open for 8% -> 10% of each run, Pallas kernels for 0% -> 0%
where the time goes in v1:
time: 562 us; the launch traced here: 560 us
  waiting for transfers between devices  312 us (56%)
  blocking collectives  68.6 us (12%)
  local copies, waits for them, and re-layouts  67.2 us (12%)
  matrix products  45.4 us (8%)
  other arithmetic  28.9 us (5%)
  starting transfers between devices  21.6 us (4%)
  between operations  16.1 us (3%)
    all_gather x1, waiting for transfers between devices, touch_the_racks(): r1 = jnp.sum(jax.lax.all_gather(field, ax_name), axis=0)  114 us
    all_gather x1, waiting for transfers between devices, shards(): frame_grad = lax.all_gather(frame_grad, 'fsdp', axis=1, tiled=True)  67.1 us
    psum x1, waiting for transfers between devices, shards(): lax.psum(contract_leading(take_own, grad_full).astype(jnp.bfloat16), 'grp')  36.7 us
    ppermute x2, waiting for transfers between devices, shards(): lax.ppermute(lax.dynamic_slice_in_dim(frozen, j * cols, cols, 0), plane,...  34 us
    psum x1, waiting for transfers between devices, shards(): down_sum, up_sum = lax.psum((down_part, up_part), 'grp')  33.4 us
    all_gather x1, blocking collectives, shards(): lora_plane = lax.all_gather(lora_tok, 'fsdp', axis=0, tiled=True)  32.5 us
    unnamed x29, local copies, waits for them, and re-layouts  29.2 us
    all_gather x1, waiting for transfers between devices, shards(): lax.all_gather(jnp.concatenate([down_sum, up_sum.reshape(-1, rank)], axis...  26 us
  transfers between devices with their start and end apart: 12, of which 6 were waited for; matrix products, arithmetic and copies ran while one was open for 10% of the time, Pallas kernels for 0%

profile of v1, /device:TPU:0, one launch (start us, length us, event | category | flops | bytes accessed | tf_op | source)
XLA Modules:
  0.0 559.8 jit_solution(13767436401614058581)
XLA Ops:
  9.6 9.7 %all-gather = s32[8,4,4]{2,1,0:T(4,128)S(1)} all-gather(s32[2,4,4]{2,1,0:T(4,128)S(1)} %pad_add_fusion), channel_id=2, replica_groups=mesh['grp'=4,'fsdp'=4,'tp'=2] {'fsdp'}, dimensions={0}, use_global_device_ids=true | all-gather | bytes 640 | tf_op jit(solution)/shard_map/all_gather | solution.py:67
  27.2 36.7 %all-reduce.4.cloned.1.call-done = bf16[192,1024]{1,0:T(8,128)(2,1)} async-done(((bf16[192,1024]{1,0:T(8,128)(2,1)}), bf16[192,1024]{1,0:T(8,128)(2,1)}) %all-reduce.4.cloned.1.call-update) | async-done | bytes 393232 | tf_op jit(solution)/shard_map/psum | solution.py:121
  64.0 5.9 %fusion.12 = bf16[768,1024]{0,1:T(8,128)(2,1)} fusion(bf16[768,1280]{1,0:T(8,128)(2,1)} %all-gather.9.cloned.1.call-done, bf16[1280,4096]{1,0:T(8,128)(2,1)} %param.13, s32[]{:T(128)S(6)} %select_n.60), kind=kOutput, calls=%fused_computation.20 | convolution fusion | flops 2014052352 | bytes 6160388 | tf_op jit(solution)/shard_map/dot_general | solution.py:127
  71.4 9.5 %collective-permute-start = (bf16[1024,512]{1,0:T(8,128)(2,1)}, bf16[1024,512]{1,0:T(8,128)(2,1)}, u32[]{:S(2)}, u32[]{:S(2)}) collective-permute-start(bf16[1024,512]{1,0:T(8,128)(2,1)} %get-tuple-element.32), channel_id=1, source_target_pairs={{0,0},{1,2},{2,4},{3,6},{4,1},{5,3},{6,5},{7,7},{8,8},{9,10},{10,1... | collective-permute-start | bytes 3145736 | tf_op jit(solution)/shard_map/ppermute | solution.py:80
  86.7 4.6 all-to-all-start
  98.8 34.0 %collective-permute-done.1 = bf16[1024,512]{1,0:T(8,128)(2,1)S(1)} collective-permute-done((bf16[1024,512]{1,0:T(8,128)(2,1)S(1)}, bf16[1024,512]{1,0:T(8,128)(2,1)S(1)}, u32[]{:S(2)}, u32[]{:S(2)}) %collective-permute-start.1) | collective-permute-done | bytes 1048608 | tf_op jit(solution)/shard_map/ppermute | solution.py:80
  133.9 4.5 fusion.16
  138.5 114.3 %all-gather.15.cloned.1.call-done = bf16[3072,1024]{0,1:T(8,128)(2,1)} async-done(((bf16[768,1024]{0,1:T(8,128)(2,1)}), bf16[3072,1024]{0,1:T(8,128)(2,1)}) %all-gather.15.cloned.1.call-update) | async-done | bytes 6291472 | tf_op jit(solution)/shard_map/all_gather | solution.py:13
  252.7 12.3 %reshape.73 = bf16[4,768,1024]{1,0,2:T(4,128)(2,1)} reshape(bf16[3072,1024]{0,1:T(8,128)(2,1)} %all-gather.15.cloned.1.call-done) | data formatting | bytes 12582912 | tf_op jit(solution)/shard_map/all_gather | solution.py:13
  265.1 10.4 %reduce_sum.108 = bf16[768,1024]{0,1:T(8,128)(2,1)S(1)} reduce(bf16[4,768,1024]{1,0,2:T(4,128)(2,1)} %reshape.73, bf16[]{:T(256)} %constant.63.clone.1), dimensions={0}, to_apply=%region_6.7 | reduce | flops 2359296 | bytes 7864322 | tf_op jit(solution)/shard_map/reduce_sum | solution.py:13
  276.5 5.3 multiply_reduce_fusion
  281.8 5.3 fusion.2
  287.1 24.1 %psum.29 = f32[2560]{0:T(1024)S(1)} all-reduce(f32[2560]{0:T(1024)S(1)} %pad_maximum_fusion.3), channel_id=1, replica_groups=mesh['grp'=4,'fsdp'=4,'tp'=2] {'fsdp','tp'}, use_global_device_ids=true, to_apply=%region_12.13 | all-reduce | flops 2560 | bytes 20480 | tf_op jit(solution)/shard_map/psum | solution.py:138
  315.7 5.3 add_convert_fusion
  321.0 4.5 reshape.66
  325.5 6.2 %copy.66 = bf16[4,256,2,512]{1,3,2,0:T(8,128)(2,1)} copy(bf16[4,256,2,512]{3,2,1,0:T(2,128)(2,1)} %reshape.66) | data formatting | bytes 4194304 | tf_op jit(solution)/shard_map/reshape | solution.py:164
  334.8 4.4 all-to-all-start.1
  339.5 32.5 %all_gather.41 = bf16[1024,64]{0,1:T(8,128)(2,1)S(1)} all-gather(bf16[256,64]{0,1:T(8,128)(2,1)S(1)} %fusion.17), channel_id=1, replica_groups=mesh['grp'=4,'fsdp'=4,'tp'=2] {'fsdp'}, dimensions={0}, use_global_device_ids=true | all-gather | bytes 163840 | tf_op jit(solution)/shard_map/all_gather | solution.py:120
  376.6 33.4 %all-reduce.6.cloned.1.call-done = (f32[512,64]{0,1:T(8,128)}, f32[1024,64]{0,1:T(8,128)}) async-done(((f32[512,64]{0,1:T(8,128)}, f32[1024,64]{0,1:T(8,128)}), (f32[512,64]{0,1:T(8,128)}, f32[1024,64]{0,1:T(8,128)})) %all-reduce.6.cloned.1.call-update) | async-done | bytes 393232 | tf_op jit(solution)/shard_map/psum | solution.py:179
  411.9 3.7 fusion.6
  416.4 26.0 %all-gather.17.cloned.1.call-done = f32[6144,64]{0,1:T(8,128)} async-done(((f32[1536,64]{0,1:T(8,128)}), f32[6144,64]{0,1:T(8,128)}) %all-gather.17.cloned.1.call-update) | async-done | bytes 1572880 | tf_op jit(solution)/shard_map/all_gather | solution.py:180
  447.7 67.1 %all-gather.13.cloned.1.call-done = bf16[768,4096]{1,0:T(8,128)(2,1)} async-done(((bf16[768,1024]{1,0:T(8,128)(2,1)}), bf16[768,4096]{1,0:T(8,128)(2,1)}) %all-gather.13.cloned.1.call-update) | async-done | bytes 6291472 | tf_op jit(solution)/shard_map/all_gather | solution.py:156
  514.8 15.0 %convolution_bitcast_fusion = f32[1280,4096]{0,1:T(8,128)} fusion(bf16[768,4096]{1,0:T(8,128)(2,1)} %all-gather.13.cloned.1.call-done, bf16[768,1280]{1,0:T(8,128)(2,1)} %all-gather.9.cloned.1.call-done), kind=kOutput, calls=%fused_computation | convolution fusion | flops 8053063680 | bytes 29229056 | tf_op jit(solution)/shard_map/dot_general | solution.py:21
  529.7 22.4 %copy.70 = f32[1280,4096]{1,0:T(8,128)} copy(f32[1280,4096]{0,1:T(8,128)} %convolution_bitcast_fusion) | data formatting | bytes 41943040
  (99 shorter events, 46.8 us)
Async XLA Ops:
  8.0 85.3 %copy-start = (bf16[2048,64]{0,1:T(8,128)(2,1)S(1)}, bf16[2048,64]{0,1:T(8,128)(2,1)}, u32[]{:S(2)}) copy-start(bf16[2048,64]{0,1:T(8,128)(2,1)} %param.17) | copy-start | bytes 786436
  8.0 55.9 %all-reduce.4.cloned.1.call-start = ((), (), s32[]{:S(2)}) async-start(), calls=%async_computation.3 | async-start | bytes 786432 | tf_op jit(solution)/shard_map/psum | solution.py:121
  21.7 0.7 copy-start.7
  25.5 108.4 %copy-start.4 = (bf16[320,1024]{1,0:T(8,128)(2,1)}, bf16[320,1024]{1,0:T(8,128)(2,1)S(1)}, u32[]{:S(2)}) copy-start(bf16[320,1024]{1,0:T(8,128)(2,1)S(1)} %all_gather.38) | copy-start | bytes 1966084
  26.6 37.4 %all-gather.9.cloned.1.call-start = ((), (), s32[]{:S(2)}) async-start(), calls=%async_computation.2 | async-start | bytes 2457600 | tf_op jit(solution)/shard_map/all_gather | solution.py:66
  27.2 106.8 %all-gather.11.cloned.1.call-start = ((), (), s32[]{:S(2)}) async-start(), calls=%async_computation.4 | async-start | bytes 1966080 | tf_op jit(solution)/shard_map/all_gather | solution.py:122
  63.9 188.8 %all-gather.15.cloned.1.call-start = ((), (), s32[]{:S(2)}) async-start(), calls=%async_computation.6 | async-start | bytes 7864320 | tf_op jit(solution)/shard_map/all_gather | solution.py:13
  64.0 5.9 %copy-start.9 = (bf16[2048,512]{1,0:T(8,128)(2,1)S(1)}, bf16[2048,512]{1,0:T(8,128)(2,1)}, u32[]{:S(2)}) copy-start(bf16[2048,512]{1,0:T(8,128)(2,1)} %param.16) | copy-start | bytes 6291460
  71.4 23.4 %collective-permute-start = (bf16[1024,512]{1,0:T(8,128)(2,1)}, bf16[1024,512]{1,0:T(8,128)(2,1)}, u32[]{:S(2)}, u32[]{:S(2)}) collective-permute-start(bf16[1024,512]{1,0:T(8,128)(2,1)} %get-tuple-element.32), channel_id=1, source_target_pairs={{0,0},{1,2},{2,4},{3,6},{4,1},{5,3},{6,5},{7,7},{8,8},{9,10},{10,1... | collective-permute-start | bytes 3145736 | tf_op jit(solution)/shard_map/ppermute | solution.py:80
  86.7 4.6 copy-start.11
  86.7 189.8 %all-to-all-start = ((bf16[4,256,1024]{2,1,0:T(8,128)(2,1)}), bf16[4,256,1024]{2,1,0:T(8,128)(2,1)}, u32[]{:S(2)}, u32[]{:S(2)}) async-start(bf16[4,256,1024]{2,1,0:T(8,128)(2,1)} %bitcast.6), calls=%async_computation | async-start | bytes 4194304 | tf_op jit(solution)/shard_map/all_to_all | solution.py:68
  91.3 41.5 %collective-permute-start.1 = (bf16[1024,512]{1,0:T(8,128)(2,1)S(1)}, bf16[1024,512]{1,0:T(8,128)(2,1)S(1)}, u32[]{:S(2)}, u32[]{:S(2)}) collective-permute-start(bf16[1024,512]{1,0:T(8,128)(2,1)S(1)} %copy-done.11), channel_id=1, source_target_pairs={{0,2},{1,0},{2,6},{3,4},{4,3},{5,1},{6,7},{7,5},{8,10},{9,8},{10,1... | collective-permute-start | bytes 3145736 | tf_op jit(solution)/shard_map/ppermute | solution.py:80
  93.3 40.6 %collective-permute-start.2 = (bf16[1024,64]{0,1:T(8,128)(2,1)S(1)}, bf16[1024,64]{0,1:T(8,128)(2,1)S(1)}, u32[]{:S(2)}, u32[]{:S(2)}) collective-permute-start(bf16[1024,64]{0,1:T(8,128)(2,1)S(1)} %constant_dynamic-slice_fusion.2), channel_id=1, source_target_pairs={{0,0},{1,2},{2,4},{3,6},{4,1},{5,3},{6,5},{7,7},{8,8},{9,10},{10,1... | collective-permute-start | bytes 393224 | tf_op jit(solution)/shard_map/ppermute | solution.py:87
  276.5 5.3 copy-start.2
  276.5 5.3 copy-start.6
  276.5 5.3 copy-start.10
  313.9 1.1 copy-start.5
  334.8 38.4 %all-to-all-start.1 = ((bf16[8,256,576]{1,2,0:T(8,128)(2,1)}), bf16[8,256,576]{1,2,0:T(8,128)(2,1)}, u32[]{:S(2)}, u32[]{:S(2)}) async-start(bf16[8,256,576]{1,2,0:T(8,128)(2,1)} %bitcast.62), calls=%async_computation.1 | async-start | bytes 4718592 | tf_op jit(solution)/shard_map/all_to_all | solution.py:173
  339.2 70.8 %all-reduce.6.cloned.1.call-start = ((), (), s32[]{:S(2)}) async-start(), calls=%async_computation.8 | async-start | bytes 786432 | tf_op jit(solution)/shard_map/psum | solution.py:179
  372.0 3.4 copy-start.8
  373.2 38.6 %copy-start.3 = (bf16[768,1024]{1,0:T(8,128)(2,1)S(1)}, bf16[768,1024]{1,0:T(8,128)(2,1)}, u32[]{:S(2)}) copy-start(bf16[768,1024]{1,0:T(8,128)(2,1)} %copy-done.2) | copy-start | bytes 4718596
  376.6 65.8 %all-gather.17.cloned.1.call-start = ((), (), s32[]{:S(2)}) async-start(), calls=%async_computation.7 | async-start | bytes 1966080 | tf_op jit(solution)/shard_map/all_gather | solution.py:180
  411.8 103.0 %all-gather.13.cloned.1.call-start = ((), (), s32[]{:S(2)}) async-start(), calls=%async_computation.5 | async-start | bytes 7864320 | tf_op jit(solution)/shard_map/all_gather | solution.py:156
  529.7 22.4 %copy-start.1 = (bf16[2048,64]{0,1:T(8,128)(2,1)S(1)}, bf16[2048,64]{0,1:T(8,128)(2,1)}, u32[]{:S(2)}) copy-start(bf16[2048,64]{0,1:T(8,128)(2,1)} %param.17) | copy-start | bytes 786436
Sparse Core Ops, SparseCore 0:
  26.7 37.1 all-reduce.3
  376.7 33.2 all-reduce.5
Sparse Core Ops, SparseCore 1:
  28.9 34.2 all-gather.8
  64.9 56.6 all-gather.10
  123.6 129.1 all-gather.14
  411.9 30.5 all-gather.16
  444.8 69.9 all-gather.12
